TPU v7x, 128 devices: a whole 4x4x4 slice. The times are simulated.
128 devices in a mesh: genes: 64 (over z, y, x_hi, core), cols: 2 (over x_lo).
Axes of the slice: x: 4 (x_hi: 2, x_lo: 2; x = x_hi * 2 + x_lo), y: 4, z: 4, core: 2. Of those that a mesh axis runs over, the one named last changes fastest.
Arguments:
- expression: float32 [384, 40960], P(None, ('genes', 'cols')), may hold values from -200 to 200
- resample: int32 [384], replicated, may hold values from 0 to 383
- labels: int32 [40960, 300], P(('genes', 'cols')), may hold values from 0 to 1, as said below
- ref_kim: float32 [40960], P(('genes', 'cols')), may hold values from 0 to 1
Outputs:
- connectivity: float32 [40960, 300], P(('genes', 'cols'))
- preservation: float32 [2, 300], replicated
Inputs may be any that keep to these rules, and one draw needn't show every extreme that they name: `labels`: each row holds exactly one 1; every module has 32 or more genes.
All inputs are finite; a program needn't handle non-finite values.
Results may differ from a plain program's by a relative error of at most 0.0031.
Values may be sent and summed in bfloat16 or wider, within the bound.
A program may use at most 64 MiB of HBM per device.

v0:
```python
import math
import jax
import jax.numpy as jnp
from jax import lax
from jax.sharding import Mesh
from jax.sharding import PartitionSpec as P

G = 40960
GENES = ("genes_0", "genes_1", "genes_2", "genes_3")
GENES_COLS = ("genes_0", "genes_1", "genes_2", "genes_3", "cols")


def in_order(blocks, dim):
    lengths = list(blocks.shape[1:])
    lengths[dim] *= blocks.shape[0]
    return jnp.moveaxis(blocks, 0, dim).reshape(lengths)


def sent_to_all(x, axis):
    copies = jnp.broadcast_to(x, (lax.axis_size(axis), *x.shape))
    return lax.all_to_all(copies, axis, split_axis=0, concat_axis=0, tiled=True)


def gathered_copies(x, axis, dim):
    return in_order(sent_to_all(x, axis), dim)


def split_up(x, dim, count):
    before, after = (x.shape[:dim], x.shape[dim + 1 :])
    return jnp.moveaxis(x.reshape(*before, count, -1, *after), dim, 0)


def sum_at_owner(x, axis, dim):
    count = lax.axis_size(axis)
    blocks = lax.all_to_all(split_up(x, dim, count), axis, 0, 0, tiled=True)
    return jnp.sum(blocks.astype(jnp.float32), axis=0)


def one_axis_at_a_time(x, axes):
    for axis in axes:
        x = lax.psum(x, axis)
    return x


def standardize(expression, resample):
    boot = jnp.take(expression, resample, axis=0)
    centered = boot - jnp.mean(boot, axis=0, keepdims=True)
    total = jnp.sum(centered * centered, axis=0, keepdims=True)
    return (centered * lax.rsqrt(total + 1e-06)).astype(jnp.bfloat16)


def local_sums(connectivity, labels, ref_kim):
    member = labels.astype(jnp.float32)
    kim = jnp.sum(connectivity * member, axis=1)
    rowsum = jnp.sum(connectivity, axis=1)
    stacked = jnp.stack(
        [kim, kim * kim, ref_kim, ref_kim * ref_kim, kim * ref_kim, rowsum, jnp.ones_like(kim)],
        axis=1,
    )
    return jnp.dot(
        member.T, stacked, precision=lax.Precision.HIGHEST, preferred_element_type=jnp.float32
    )


def preserve(sums, total_genes):
    counts = sums[:, 6]
    mean_x = sums[:, 0] / (counts * counts)
    var_x = jnp.maximum(sums[:, 1] / (counts * counts * counts) - mean_x * mean_x, 0.0001)
    mean_y = sums[:, 2] / counts
    var_y = jnp.maximum(sums[:, 3] / counts - mean_y * mean_y, 0.01)
    cross = sums[:, 4] / (counts * counts) - mean_x * mean_y
    between = (sums[:, 5] - sums[:, 0]) / (counts * (total_genes - counts))
    density = (mean_x - between) * jnp.sqrt(counts / var_x)
    linked = cross * jnp.sqrt(counts / (var_x * var_y))
    return jnp.stack([density, linked], axis=0)


def tile_term(row_block, column_block, column_ids, module_count):
    scores = lax.dot_general(
        row_block, column_block, (((0,), (0,)), ((), ())), preferred_element_type=jnp.float32
    )
    squares = scores * scores
    adjacency = (squares * squares * squares).astype(jnp.bfloat16)
    member_block = (
        column_ids[:, None] == jnp.arange(module_count, dtype=jnp.int32)[None, :]
    ).astype(jnp.bfloat16)
    return jnp.dot(adjacency, member_block, preferred_element_type=jnp.float32)


def add_tiles(carried, row_block, piece, every_ids, shard_width, module_count):
    span_width = piece.shape[1]
    column_step = shard_width * math.gcd(span_width // shard_width, 8)
    steps_total = span_width // column_step

    def one_step(step_index, accumulated):
        columns = lax.dynamic_slice_in_dim(piece, step_index * column_step, column_step, 1)
        column_ids = lax.dynamic_slice_in_dim(every_ids, step_index * column_step, column_step, 0)
        return accumulated + tile_term(row_block, columns, column_ids, module_count)

    return lax.fori_loop(0, steps_total, one_step, carried)


def local(expression, resample, labels, ref_kim):
    scaled = standardize(expression, resample)
    module_count = labels.shape[1]
    shard_width = scaled.shape[1]
    module_ids = jnp.sum(labels * jnp.arange(module_count, dtype=jnp.int32)[None, :], axis=1)
    row_block = gathered_copies(scaled, "cols", 1)
    panel_ids = gathered_copies(module_ids, GENES, 0)
    initial = jnp.zeros((row_block.shape[1], module_count), jnp.float32)
    partial_value = add_tiles(
        initial,
        row_block,
        lax.all_gather(scaled, GENES, axis=1, tiled=True),
        panel_ids,
        shard_width,
        module_count,
    )
    connectivity = sum_at_owner(partial_value.astype(jnp.bfloat16), "cols", 0)
    sums = one_axis_at_a_time(local_sums(connectivity, labels, ref_kim), GENES_COLS)
    return (connectivity, preserve(sums, G))


def solution(mesh):
    torus = Mesh(
        mesh.devices.reshape(4, 4, 2, 2, mesh.shape["cols"]),
        ("genes_0", "genes_1", "genes_2", "genes_3", "cols"),
    )
    placed = (P(None, GENES_COLS), P(), P(GENES_COLS, None), P(GENES_COLS))
    return jax.shard_map(
        local, mesh=torus, in_specs=placed, out_specs=(P(GENES_COLS, None), P()), check_vma=False
    )
```

profile of v0, /device:TPU:2, one launch (start us, length us, event | category | flops | bytes accessed | tf_op | source)
XLA Modules:
  0.0 233.6 jit_solution(9748620751659558973)
XLA Ops:
  7.2 0.0 copy-start
  7.2 0.0 all-gather.2.cloned.1.call-start
  7.2 0.7 compare_select_fusion
  8.0 0.7 compare_and_fusion
  8.6 1.3 copy.21
  9.9 1.7 gather_fusion
  11.7 0.2 copy.22
  11.9 0.2 select_reduce_fusion
  12.0 0.2 multiply_reduce_fusion
  12.3 0.9 multiply_convert_fusion
  13.1 0.0 all-gather.2.cloned.1.call-update
  13.2 0.0 copy-done
  13.2 0.1 multiply_reduce_fusion.2
  13.2 0.1 broadcast_in_dim.35
  13.3 20.1 %all_to_all.16 = s32[64,1,320]{2,1,0:T(1,128)S(1)} all-to-all(s32[64,1,320]{2,1,0:T(1,128)S(1)} %broadcast_in_dim.35), channel_id=1, replica_groups=mesh['genes_0'=4,'genes_1'=4,'genes_2'=2,'genes_3'=2,'cols'=2] {'genes_0..., dimensions={0} | all-to-all | bytes 163840 | tf_op jit(solution)/shard_map/all_to_all | solution.py:21
  33.4 1.8 broadcast_in_dim.34
  35.1 4.9 %all-to-all-start = ((bf16[2,384,320]{1,2,0:T(8,128)(2,1)}), bf16[2,384,320]{1,2,0:T(8,128)(2,1)S(1)}, u32[]{:S(2)}, u32[]{:S(2)}) async-start(bf16[2,384,320]{1,2,0:T(8,128)(2,1)} %broadcast_in_dim.34), calls=%async_computation | async-start | bytes 983040 | tf_op jit(solution)/shard_map/all_to_all | solution.py:21
  40.0 0.2 reduce.1
  40.3 0.1 reshape.235
  40.4 6.0 %all-to-all-done = bf16[2,384,320]{1,2,0:T(8,128)(2,1)S(1)} async-done(((bf16[2,384,320]{1,2,0:T(8,128)(2,1)}), bf16[2,384,320]{1,2,0:T(8,128)(2,1)S(1)}, u32[]{:S(2)}, u32[]{:S(2)}) %all-to-all-start) | async-done | bytes 491552 | tf_op jit(solution)/shard_map/all_to_all | solution.py:21
  46.4 0.3 copy.24
  46.6 69.9 %all-gather.2.cloned.1.call-done = bf16[384,20480]{0,1:T(8,128)(2,1)} async-done(((bf16[384,320]{0,1:T(8,128)(2,1)}), bf16[384,20480]{0,1:T(8,128)(2,1)}) %all-gather.2.cloned.1.call-update) | async-done | bytes 15728656 | tf_op jit(solution)/shard_map/all_gather | solution.py:114
  116.5 0.0 copy-start.2
  116.5 43.6 %while.14 = (s32[]{:T(128)}, f32[640,300]{0,1:T(8,128)S(1)}, bf16[384,20480]{0,1:T(8,128)(2,1)}, bf16[384,640]{1,0:T(8,128)(2,1)S(1)}, s32[20480]{0:T(1024)S(1)}...) while((s32[]{:T(128)}, f32[640,300]{0,1:T(8,128)S(1)}, bf16[384,20480]{0,1:T(8,128)(2,1)}, ...), condition=%wide.region_4.5_spmd.clone, body=%wide.region_3.4_spmd.clone.sunk | while | flops 2249036800 | bytes 4024477 | solution.py:100
  116.5 0.1 dynamic_slice.25
  116.6 5.3 %fusion.32 = f32[640,300]{0,1:T(8,128)S(1)} fusion(s32[2560]{0:T(1024)S(1)} %dynamic_slice.25, bf16[384,640]{1,0:T(8,128)(2,1)S(1)} %get-tuple-element.204, bf16[384,20480]{0,1:T(8,128)(2,1)} %get-tuple-element.203, s32[]{:T(128)S(6)} %select_n.27, f32[640,300]{0,1:T(8,128)S(1)} %get-tuple-element.193, pred[]{:T(512)S(6)} %compare.3), kind=kOutput, calls=%fused_computation.7.clone.1 | convolution fusion | flops 2249036800 | bytes 4003845 | tf_op jit(solution)/shard_map/while/body/eval_jaxpr/dot_general | solution.py:87
  122.0 0.1 dynamic_slice.25
  122.1 5.3 %fusion.32 = f32[640,300]{0,1:T(8,128)S(1)} fusion(s32[2560]{0:T(1024)S(1)} %dynamic_slice.25, bf16[384,640]{1,0:T(8,128)(2,1)S(1)} %get-tuple-element.204, bf16[384,20480]{0,1:T(8,128)(2,1)} %get-tuple-element.203, s32[]{:T(128)S(6)} %select_n.27, f32[640,300]{0,1:T(8,128)S(1)} %get-tuple-element.193, pred[]{:T(512)S(6)} %compare.3), kind=kOutput, calls=%fused_computation.7.clone.1 | convolution fusion | flops 2249036800 | bytes 4003845 | tf_op jit(solution)/shard_map/while/body/eval_jaxpr/dot_general | solution.py:87
  127.4 0.1 dynamic_slice.25
  127.5 5.3 %fusion.32 = f32[640,300]{0,1:T(8,128)S(1)} fusion(s32[2560]{0:T(1024)S(1)} %dynamic_slice.25, bf16[384,640]{1,0:T(8,128)(2,1)S(1)} %get-tuple-element.204, bf16[384,20480]{0,1:T(8,128)(2,1)} %get-tuple-element.203, s32[]{:T(128)S(6)} %select_n.27, f32[640,300]{0,1:T(8,128)S(1)} %get-tuple-element.193, pred[]{:T(512)S(6)} %compare.3), kind=kOutput, calls=%fused_computation.7.clone.1 | convolution fusion | flops 2249036800 | bytes 4003845 | tf_op jit(solution)/shard_map/while/body/eval_jaxpr/dot_general | solution.py:87
  132.9 0.1 dynamic_slice.25
  133.0 5.3 %fusion.32 = f32[640,300]{0,1:T(8,128)S(1)} fusion(s32[2560]{0:T(1024)S(1)} %dynamic_slice.25, bf16[384,640]{1,0:T(8,128)(2,1)S(1)} %get-tuple-element.204, bf16[384,20480]{0,1:T(8,128)(2,1)} %get-tuple-element.203, s32[]{:T(128)S(6)} %select_n.27, f32[640,300]{0,1:T(8,128)S(1)} %get-tuple-element.193, pred[]{:T(512)S(6)} %compare.3), kind=kOutput, calls=%fused_computation.7.clone.1 | convolution fusion | flops 2249036800 | bytes 4003845 | tf_op jit(solution)/shard_map/while/body/eval_jaxpr/dot_general | solution.py:87
  138.3 0.1 dynamic_slice.25
  138.4 5.3 %fusion.32 = f32[640,300]{0,1:T(8,128)S(1)} fusion(s32[2560]{0:T(1024)S(1)} %dynamic_slice.25, bf16[384,640]{1,0:T(8,128)(2,1)S(1)} %get-tuple-element.204, bf16[384,20480]{0,1:T(8,128)(2,1)} %get-tuple-element.203, s32[]{:T(128)S(6)} %select_n.27, f32[640,300]{0,1:T(8,128)S(1)} %get-tuple-element.193, pred[]{:T(512)S(6)} %compare.3), kind=kOutput, calls=%fused_computation.7.clone.1 | convolution fusion | flops 2249036800 | bytes 4003845 | tf_op jit(solution)/shard_map/while/body/eval_jaxpr/dot_general | solution.py:87
  143.8 0.1 dynamic_slice.25
  143.9 5.3 %fusion.32 = f32[640,300]{0,1:T(8,128)S(1)} fusion(s32[2560]{0:T(1024)S(1)} %dynamic_slice.25, bf16[384,640]{1,0:T(8,128)(2,1)S(1)} %get-tuple-element.204, bf16[384,20480]{0,1:T(8,128)(2,1)} %get-tuple-element.203, s32[]{:T(128)S(6)} %select_n.27, f32[640,300]{0,1:T(8,128)S(1)} %get-tuple-element.193, pred[]{:T(512)S(6)} %compare.3), kind=kOutput, calls=%fused_computation.7.clone.1 | convolution fusion | flops 2249036800 | bytes 4003845 | tf_op jit(solution)/shard_map/while/body/eval_jaxpr/dot_general | solution.py:87
  149.2 0.1 dynamic_slice.25
  149.3 5.3 %fusion.32 = f32[640,300]{0,1:T(8,128)S(1)} fusion(s32[2560]{0:T(1024)S(1)} %dynamic_slice.25, bf16[384,640]{1,0:T(8,128)(2,1)S(1)} %get-tuple-element.204, bf16[384,20480]{0,1:T(8,128)(2,1)} %get-tuple-element.203, s32[]{:T(128)S(6)} %select_n.27, f32[640,300]{0,1:T(8,128)S(1)} %get-tuple-element.193, pred[]{:T(512)S(6)} %compare.3), kind=kOutput, calls=%fused_computation.7.clone.1 | convolution fusion | flops 2249036800 | bytes 4003845 | tf_op jit(solution)/shard_map/while/body/eval_jaxpr/dot_general | solution.py:87
  154.7 0.1 dynamic_slice.25
  154.8 5.3 %fusion.32 = f32[640,300]{0,1:T(8,128)S(1)} fusion(s32[2560]{0:T(1024)S(1)} %dynamic_slice.25, bf16[384,640]{1,0:T(8,128)(2,1)S(1)} %get-tuple-element.204, bf16[384,20480]{0,1:T(8,128)(2,1)} %get-tuple-element.203, s32[]{:T(128)S(6)} %select_n.27, f32[640,300]{0,1:T(8,128)S(1)} %get-tuple-element.193, pred[]{:T(512)S(6)} %compare.3), kind=kOutput, calls=%fused_computation.7.clone.1 | convolution fusion | flops 2249036800 | bytes 4003845 | tf_op jit(solution)/shard_map/while/body/eval_jaxpr/dot_general | solution.py:87
  160.2 0.4 reshape.236
  160.6 0.8 copy.25
  161.5 5.0 %all-to-all-start.2 = ((bf16[2,320,300]{1,2,0:T(8,128)(2,1)}), bf16[2,320,300]{1,2,0:T(8,128)(2,1)S(1)}, u32[]{:S(2)}, u32[]{:S(2)}) async-start(bf16[2,320,300]{1,2,0:T(8,128)(2,1)} %copy.25), calls=%async_computation.2 | async-start | bytes 933888 | tf_op jit(solution)/shard_map/all_to_all | solution.py:35
  166.4 0.0 copy-done.2
  166.4 6.3 %all-to-all-done.2 = bf16[2,320,300]{1,2,0:T(8,128)(2,1)S(1)} async-done(((bf16[2,320,300]{1,2,0:T(8,128)(2,1)}), bf16[2,320,300]{1,2,0:T(8,128)(2,1)S(1)}, u32[]{:S(2)}, u32[]{:S(2)}) %all-to-all-start.2) | async-done | bytes 384032 | tf_op jit(solution)/shard_map/all_to_all | solution.py:35
  172.7 0.2 convert_reduce_fusion
  172.9 0.0 copy-start.1
  172.9 0.1 multiply_reduce_fusion.1
  173.1 0.4 convolution_bitcast_fusion
  173.6 17.1 %psum.35 = f32[300,7]{0,1:T(8,128)S(1)} all-reduce(f32[300,7]{0,1:T(8,128)S(1)} %convolution_bitcast_fusion), channel_id=1, replica_groups=mesh['genes_0'=4,'genes_1'=4,'genes_2'=2,'genes_3'=2,'cols'=2] {'genes_0'}, use_global_device_ids=true, to_apply=%region_8.9 | all-reduce | flops 2100 | bytes 16800 | tf_op jit(solution)/shard_map/psum | solution.py:41
  190.7 14.9 %psum.36 = f32[300,7]{0,1:T(8,128)S(1)} all-reduce(f32[300,7]{0,1:T(8,128)S(1)} %psum.35), channel_id=1, replica_groups=mesh['genes_0'=4,'genes_1'=4,'genes_2'=2,'genes_3'=2,'cols'=2] {'genes_1'}, use_global_device_ids=true, to_apply=%region_9.10 | all-reduce | flops 2100 | bytes 16800 | tf_op jit(solution)/shard_map/psum | solution.py:41
  205.6 8.2 %psum.37 = f32[300,7]{0,1:T(8,128)S(1)} all-reduce(f32[300,7]{0,1:T(8,128)S(1)} %psum.36), channel_id=1, replica_groups=mesh['genes_0'=4,'genes_1'=4,'genes_2'=2,'genes_3'=2,'cols'=2] {'genes_2'}, use_global_device_ids=true, to_apply=%region_10.11 | all-reduce | flops 2100 | bytes 16800 | tf_op jit(solution)/shard_map/psum | solution.py:41
  213.8 3.3 %psum.38 = f32[300,7]{0,1:T(8,128)S(1)} all-reduce(f32[300,7]{0,1:T(8,128)S(1)} %psum.37), channel_id=1, replica_groups=mesh['genes_0'=4,'genes_1'=4,'genes_2'=2,'genes_3'=2,'cols'=2] {'genes_3'}, use_global_device_ids=true, to_apply=%region_11.12 | all-reduce | flops 2100 | bytes 16800 | tf_op jit(solution)/shard_map/psum | solution.py:41
  217.0 9.1 %psum.39 = f32[300,7]{0,1:T(8,128)S(1)} all-reduce(f32[300,7]{0,1:T(8,128)S(1)} %psum.38), channel_id=1, replica_groups=mesh['genes_0'=4,'genes_1'=4,'genes_2'=2,'genes_3'=2,'cols'=2] {'cols'}, use_global_device_ids=true, to_apply=%region_12.13 | all-reduce | flops 2100 | bytes 16800 | tf_op jit(solution)/shard_map/psum | solution.py:41
  226.2 0.6 pad_maximum_fusion
  226.8 0.0 copy-done.1
  (16 shorter events, 0.2 us)
Async XLA Ops:
  7.2 6.0 %copy-start = (s32[320,300]{0,1:T(8,128)S(1)}, s32[320,300]{0,1:T(8,128)}, u32[]{:S(2)}) copy-start(s32[320,300]{0,1:T(8,128)} %param.8) | copy-start | bytes 1152004
  7.2 109.3 %all-gather.2.cloned.1.call-start = ((), (), s32[]{:S(2)}) async-start(), calls=%async_computation.3 | async-start | bytes 15974400 | tf_op jit(solution)/shard_map/all_gather | solution.py:114
  35.1 11.2 %all-to-all-start = ((bf16[2,384,320]{1,2,0:T(8,128)(2,1)}), bf16[2,384,320]{1,2,0:T(8,128)(2,1)S(1)}, u32[]{:S(2)}, u32[]{:S(2)}) async-start(bf16[2,384,320]{1,2,0:T(8,128)(2,1)} %broadcast_in_dim.34), calls=%async_computation | async-start | bytes 983040 | tf_op jit(solution)/shard_map/all_to_all | solution.py:21
  116.5 49.9 %copy-start.2 = (f32[320]{0:T(512)S(1)}, f32[320]{0:T(512)}, u32[]{:S(2)}) copy-start(f32[320]{0:T(512)} %param.9) | copy-start | bytes 3844
  161.5 11.2 %all-to-all-start.2 = ((bf16[2,320,300]{1,2,0:T(8,128)(2,1)}), bf16[2,320,300]{1,2,0:T(8,128)(2,1)S(1)}, u32[]{:S(2)}, u32[]{:S(2)}) async-start(bf16[2,320,300]{1,2,0:T(8,128)(2,1)} %copy.25), calls=%async_computation.2 | async-start | bytes 933888 | tf_op jit(solution)/shard_map/all_to_all | solution.py:35
  172.9 53.8 %copy-start.1 = (f32[320,300]{0,1:T(8,128)}, f32[320,300]{0,1:T(8,128)S(1)}, u32[]{:S(2)}) copy-start(f32[320,300]{0,1:T(8,128)S(1)} %get-tuple-element.136) | copy-start | bytes 1152004
Sparse Core Ops, SparseCore 0:
  13.3 103.1 all-gather.1
where the time goes:
time: 234 us
  waiting for transfers between devices  82.2 us (35%)
  blocking collectives  72.6 us (31%)
  matrix products  43.2 us (18%)
  between operations  14.2 us (6%)
  starting transfers between devices  9.89 us (4%)
  local copies, waits for them, and re-layouts  7.35 us (3%)
  other arithmetic  4.01 us (2%)
    all_gather x1, waiting for transfers between devices, local(): lax.all_gather(scaled, GENES, axis=1, tiled=True)  69.9 us
    psum x5, blocking collectives, one_axis_at_a_time(): x = lax.psum(x, axis)  52.5 us
    dot_general x8, matrix products, tile_term(): return jnp.dot(adjacency, member_block, preferred_element_type=jnp.float32)  42.8 us
    all_to_all x1, blocking collectives, sent_to_all(): return lax.all_to_all(copies, axis, split_axis=0, concat_axis=0, tiled=True)  20.1 us
    all_to_all x1, waiting for transfers between devices, sum_at_owner(): blocks = lax.all_to_all(split_up(x, dim, count), axis, 0, 0, tiled=True)  6.29 us
    all_to_all x1, waiting for transfers between devices, sent_to_all(): return lax.all_to_all(copies, axis, split_axis=0, concat_axis=0, tiled=True)  5.99 us
    all_to_all x1, starting transfers between devices, sum_at_owner(): blocks = lax.all_to_all(split_up(x, dim, count), axis, 0, 0, tiled=True)  4.95 us
    all_to_all x1, starting transfers between devices, sent_to_all(): return lax.all_to_all(copies, axis, split_axis=0, concat_axis=0, tiled=True)  4.9 us
  transfers between devices with their start and end apart: 3, of which 3 were waited for; matrix products, arithmetic and copies ran while one was open for 1% of the time, Pallas kernels for 0%

commit v1 on v0

--- a/solution.py
+++ b/solution.py
@@ -38,7 +38,7 @@
 
 def one_axis_at_a_time(x, axes):
     for axis in axes:
-        x = lax.psum(x, axis)
+        x = jnp.sum(lax.all_gather(x, axis), axis=0)
     return x
 
 

time: 234 us -> 220 us (0.940)
  blocking collectives: 72.6 us -> 56.6 us
    psum x5 -> x0, blocking collectives: 52.5 us -> none  [one_axis_at_a_time(): x = lax.psum(x, axis)]
    all_gather x0 -> x5, blocking collectives: none -> 36.5 us  [one_axis_at_a_time(): x = jnp.sum(lax.all_gather(x, axis), axis=0)]
where the time goes in v1:
time: 220 us; the launch traced here: 218 us
  waiting for transfers between devices  82.2 us (37%)
  blocking collectives  56.6 us (26%)
  matrix products  43.2 us (20%)
  between operations  14.2 us (6%)
  starting transfers between devices  9.89 us (4%)
  local copies, waits for them, and re-layouts  7.35 us (3%)
  other arithmetic  4.05 us (2%)
    all_gather x1, waiting for transfers between devices, local(): lax.all_gather(scaled, GENES, axis=1, tiled=True)  69.9 us
    dot_general x8, matrix products, tile_term(): return jnp.dot(adjacency, member_block, preferred_element_type=jnp.float32)  42.8 us
    all_gather x5, blocking collectives, one_axis_at_a_time(): x = jnp.sum(lax.all_gather(x, axis), axis=0)  36.5 us
    all_to_all x1, blocking collectives, sent_to_all(): return lax.all_to_all(copies, axis, split_axis=0, concat_axis=0, tiled=True)  20.1 us
    all_to_all x1, waiting for transfers between devices, sum_at_owner(): blocks = lax.all_to_all(split_up(x, dim, count), axis, 0, 0, tiled=True)  6.29 us
    all_to_all x1, waiting for transfers between devices, sent_to_all(): return lax.all_to_all(copies, axis, split_axis=0, concat_axis=0, tiled=True)  5.99 us
    all_to_all x1, starting transfers between devices, sum_at_owner(): blocks = lax.all_to_all(split_up(x, dim, count), axis, 0, 0, tiled=True)  4.95 us
    all_to_all x1, starting transfers between devices, sent_to_all(): return lax.all_to_all(copies, axis, split_axis=0, concat_axis=0, tiled=True)  4.9 us
  transfers between devices with their start and end apart: 3, of which 3 were waited for; matrix products, arithmetic and copies ran while one was open for 1% of the time, Pallas kernels for 0%

profile of v1, /device:TPU:2, one launch (start us, length us, event | category | flops | bytes accessed | tf_op | source)
XLA Modules:
  0.0 217.6 jit_solution(1173046854202709068)
XLA Ops:
  7.2 0.0 copy-start
  7.2 0.0 all-gather.12.cloned.1.call-start
  7.2 0.7 compare_select_fusion
  8.0 0.7 compare_and_fusion
  8.6 1.3 copy.21
  9.9 1.7 gather_fusion
  11.7 0.2 copy.22
  11.9 0.2 select_reduce_fusion
  12.0 0.2 multiply_reduce_fusion
  12.3 0.9 multiply_convert_fusion
  13.1 0.0 all-gather.12.cloned.1.call-update
  13.2 0.0 copy-done
  13.2 0.1 multiply_reduce_fusion.2
  13.2 0.1 broadcast_in_dim.35
  13.3 20.1 %all_to_all.16 = s32[64,1,320]{2,1,0:T(1,128)S(1)} all-to-all(s32[64,1,320]{2,1,0:T(1,128)S(1)} %broadcast_in_dim.35), channel_id=1, replica_groups=mesh['genes_0'=4,'genes_1'=4,'genes_2'=2,'genes_3'=2,'cols'=2] {'genes_0..., dimensions={0} | all-to-all | bytes 163840 | tf_op jit(solution)/shard_map/all_to_all | solution.py:21
  33.4 1.8 broadcast_in_dim.34
  35.1 4.9 %all-to-all-start = ((bf16[2,384,320]{1,2,0:T(8,128)(2,1)}), bf16[2,384,320]{1,2,0:T(8,128)(2,1)S(1)}, u32[]{:S(2)}, u32[]{:S(2)}) async-start(bf16[2,384,320]{1,2,0:T(8,128)(2,1)} %broadcast_in_dim.34), calls=%async_computation | async-start | bytes 983040 | tf_op jit(solution)/shard_map/all_to_all | solution.py:21
  40.0 0.2 reduce.6
  40.3 0.1 reshape.235
  40.4 6.0 %all-to-all-done = bf16[2,384,320]{1,2,0:T(8,128)(2,1)S(1)} async-done(((bf16[2,384,320]{1,2,0:T(8,128)(2,1)}), bf16[2,384,320]{1,2,0:T(8,128)(2,1)S(1)}, u32[]{:S(2)}, u32[]{:S(2)}) %all-to-all-start) | async-done | bytes 491552 | tf_op jit(solution)/shard_map/all_to_all | solution.py:21
  46.4 0.3 copy.24
  46.6 69.9 %all-gather.12.cloned.1.call-done = bf16[384,20480]{0,1:T(8,128)(2,1)} async-done(((bf16[384,320]{0,1:T(8,128)(2,1)}), bf16[384,20480]{0,1:T(8,128)(2,1)}) %all-gather.12.cloned.1.call-update) | async-done | bytes 15728656 | tf_op jit(solution)/shard_map/all_gather | solution.py:114
  116.5 0.0 copy-start.2
  116.5 43.6 %while.14 = (s32[]{:T(128)}, f32[640,300]{0,1:T(8,128)S(1)}, bf16[384,20480]{0,1:T(8,128)(2,1)}, bf16[384,640]{1,0:T(8,128)(2,1)S(1)}, s32[20480]{0:T(1024)S(1)}...) while((s32[]{:T(128)}, f32[640,300]{0,1:T(8,128)S(1)}, bf16[384,20480]{0,1:T(8,128)(2,1)}, ...), condition=%wide.region_4.5_spmd.clone, body=%wide.region_3.4_spmd.clone.sunk | while | flops 2249036800 | bytes 4024477 | solution.py:100
  116.5 0.1 dynamic_slice.25
  116.6 5.3 %fusion.32 = f32[640,300]{0,1:T(8,128)S(1)} fusion(s32[2560]{0:T(1024)S(1)} %dynamic_slice.25, bf16[384,640]{1,0:T(8,128)(2,1)S(1)} %get-tuple-element.204, bf16[384,20480]{0,1:T(8,128)(2,1)} %get-tuple-element.203, s32[]{:T(128)S(6)} %select_n.27, f32[640,300]{0,1:T(8,128)S(1)} %get-tuple-element.193, pred[]{:T(512)S(6)} %compare.3), kind=kOutput, calls=%fused_computation.7.clone.1 | convolution fusion | flops 2249036800 | bytes 4003845 | tf_op jit(solution)/shard_map/while/body/eval_jaxpr/dot_general | solution.py:87
  122.0 0.1 dynamic_slice.25
  122.1 5.3 %fusion.32 = f32[640,300]{0,1:T(8,128)S(1)} fusion(s32[2560]{0:T(1024)S(1)} %dynamic_slice.25, bf16[384,640]{1,0:T(8,128)(2,1)S(1)} %get-tuple-element.204, bf16[384,20480]{0,1:T(8,128)(2,1)} %get-tuple-element.203, s32[]{:T(128)S(6)} %select_n.27, f32[640,300]{0,1:T(8,128)S(1)} %get-tuple-element.193, pred[]{:T(512)S(6)} %compare.3), kind=kOutput, calls=%fused_computation.7.clone.1 | convolution fusion | flops 2249036800 | bytes 4003845 | tf_op jit(solution)/shard_map/while/body/eval_jaxpr/dot_general | solution.py:87
  127.4 0.1 dynamic_slice.25
  127.5 5.3 %fusion.32 = f32[640,300]{0,1:T(8,128)S(1)} fusion(s32[2560]{0:T(1024)S(1)} %dynamic_slice.25, bf16[384,640]{1,0:T(8,128)(2,1)S(1)} %get-tuple-element.204, bf16[384,20480]{0,1:T(8,128)(2,1)} %get-tuple-element.203, s32[]{:T(128)S(6)} %select_n.27, f32[640,300]{0,1:T(8,128)S(1)} %get-tuple-element.193, pred[]{:T(512)S(6)} %compare.3), kind=kOutput, calls=%fused_computation.7.clone.1 | convolution fusion | flops 2249036800 | bytes 4003845 | tf_op jit(solution)/shard_map/while/body/eval_jaxpr/dot_general | solution.py:87
  132.9 0.1 dynamic_slice.25
  133.0 5.3 %fusion.32 = f32[640,300]{0,1:T(8,128)S(1)} fusion(s32[2560]{0:T(1024)S(1)} %dynamic_slice.25, bf16[384,640]{1,0:T(8,128)(2,1)S(1)} %get-tuple-element.204, bf16[384,20480]{0,1:T(8,128)(2,1)} %get-tuple-element.203, s32[]{:T(128)S(6)} %select_n.27, f32[640,300]{0,1:T(8,128)S(1)} %get-tuple-element.193, pred[]{:T(512)S(6)} %compare.3), kind=kOutput, calls=%fused_computation.7.clone.1 | convolution fusion | flops 2249036800 | bytes 4003845 | tf_op jit(solution)/shard_map/while/body/eval_jaxpr/dot_general | solution.py:87
  138.3 0.1 dynamic_slice.25
  138.4 5.3 %fusion.32 = f32[640,300]{0,1:T(8,128)S(1)} fusion(s32[2560]{0:T(1024)S(1)} %dynamic_slice.25, bf16[384,640]{1,0:T(8,128)(2,1)S(1)} %get-tuple-element.204, bf16[384,20480]{0,1:T(8,128)(2,1)} %get-tuple-element.203, s32[]{:T(128)S(6)} %select_n.27, f32[640,300]{0,1:T(8,128)S(1)} %get-tuple-element.193, pred[]{:T(512)S(6)} %compare.3), kind=kOutput, calls=%fused_computation.7.clone.1 | convolution fusion | flops 2249036800 | bytes 4003845 | tf_op jit(solution)/shard_map/while/body/eval_jaxpr/dot_general | solution.py:87
  143.8 0.1 dynamic_slice.25
  143.9 5.3 %fusion.32 = f32[640,300]{0,1:T(8,128)S(1)} fusion(s32[2560]{0:T(1024)S(1)} %dynamic_slice.25, bf16[384,640]{1,0:T(8,128)(2,1)S(1)} %get-tuple-element.204, bf16[384,20480]{0,1:T(8,128)(2,1)} %get-tuple-element.203, s32[]{:T(128)S(6)} %select_n.27, f32[640,300]{0,1:T(8,128)S(1)} %get-tuple-element.193, pred[]{:T(512)S(6)} %compare.3), kind=kOutput, calls=%fused_computation.7.clone.1 | convolution fusion | flops 2249036800 | bytes 4003845 | tf_op jit(solution)/shard_map/while/body/eval_jaxpr/dot_general | solution.py:87
  149.2 0.1 dynamic_slice.25
  149.3 5.3 %fusion.32 = f32[640,300]{0,1:T(8,128)S(1)} fusion(s32[2560]{0:T(1024)S(1)} %dynamic_slice.25, bf16[384,640]{1,0:T(8,128)(2,1)S(1)} %get-tuple-element.204, bf16[384,20480]{0,1:T(8,128)(2,1)} %get-tuple-element.203, s32[]{:T(128)S(6)} %select_n.27, f32[640,300]{0,1:T(8,128)S(1)} %get-tuple-element.193, pred[]{:T(512)S(6)} %compare.3), kind=kOutput, calls=%fused_computation.7.clone.1 | convolution fusion | flops 2249036800 | bytes 4003845 | tf_op jit(solution)/shard_map/while/body/eval_jaxpr/dot_general | solution.py:87
  154.7 0.1 dynamic_slice.25
  154.8 5.3 %fusion.32 = f32[640,300]{0,1:T(8,128)S(1)} fusion(s32[2560]{0:T(1024)S(1)} %dynamic_slice.25, bf16[384,640]{1,0:T(8,128)(2,1)S(1)} %get-tuple-element.204, bf16[384,20480]{0,1:T(8,128)(2,1)} %get-tuple-element.203, s32[]{:T(128)S(6)} %select_n.27, f32[640,300]{0,1:T(8,128)S(1)} %get-tuple-element.193, pred[]{:T(512)S(6)} %compare.3), kind=kOutput, calls=%fused_computation.7.clone.1 | convolution fusion | flops 2249036800 | bytes 4003845 | tf_op jit(solution)/shard_map/while/body/eval_jaxpr/dot_general | solution.py:87
  160.2 0.4 reshape.236
  160.6 0.8 copy.25
  161.5 5.0 %all-to-all-start.2 = ((bf16[2,320,300]{1,2,0:T(8,128)(2,1)}), bf16[2,320,300]{1,2,0:T(8,128)(2,1)S(1)}, u32[]{:S(2)}, u32[]{:S(2)}) async-start(bf16[2,320,300]{1,2,0:T(8,128)(2,1)} %copy.25), calls=%async_computation.2 | async-start | bytes 933888 | tf_op jit(solution)/shard_map/all_to_all | solution.py:35
  166.4 0.0 copy-done.2
  166.4 6.3 %all-to-all-done.2 = bf16[2,320,300]{1,2,0:T(8,128)(2,1)S(1)} async-done(((bf16[2,320,300]{1,2,0:T(8,128)(2,1)}), bf16[2,320,300]{1,2,0:T(8,128)(2,1)S(1)}, u32[]{:S(2)}, u32[]{:S(2)}) %all-to-all-start.2) | async-done | bytes 384032 | tf_op jit(solution)/shard_map/all_to_all | solution.py:35
  172.7 0.2 convert_reduce_fusion
  172.9 0.0 copy-start.1
  172.9 0.1 multiply_reduce_fusion.1
  173.1 0.4 convolution_bitcast_fusion
  173.6 12.5 %all-gather.5 = f32[4,300,7]{1,2,0:T(8,128)S(1)} all-gather(f32[1,300,7]{1,2,0:T(8,128)S(1)} %convolution_bitcast_fusion), channel_id=2, replica_groups=mesh['genes_0'=4,'genes_1'=4,'genes_2'=2,'genes_3'=2,'cols'=2] {'genes_0'}, dimensions={0}, use_global_device_ids=true | all-gather | bytes 42000 | tf_op jit(solution)/shard_map/all_gather | solution.py:41
  186.0 11.9 %all-gather.6 = f32[4,300,7]{1,2,0:T(8,128)S(1)} all-gather(f32[1,300,7]{1,2,0:T(8,128)S(1)} %bitcast.89), channel_id=3, replica_groups=mesh['genes_0'=4,'genes_1'=4,'genes_2'=2,'genes_3'=2,'cols'=2] {'genes_1'}, dimensions={0}, use_global_device_ids=true | all-gather | bytes 42000 | tf_op jit(solution)/shard_map/all_gather | solution.py:41
  198.0 5.9 %all-gather.7 = f32[2,300,7]{1,2,0:T(8,128)S(1)} all-gather(f32[1,300,7]{1,2,0:T(8,128)S(1)} %bitcast.88), channel_id=4, replica_groups=mesh['genes_0'=4,'genes_1'=4,'genes_2'=2,'genes_3'=2,'cols'=2] {'genes_2'}, dimensions={0}, use_global_device_ids=true | all-gather | bytes 25200 | tf_op jit(solution)/shard_map/all_gather | solution.py:41
  203.9 1.8 all-gather.8
  205.7 4.4 %all-gather.9 = f32[2,300,7]{1,2,0:T(8,128)S(1)} all-gather(f32[1,300,7]{1,2,0:T(8,128)S(1)} %bitcast.87), channel_id=6, replica_groups=mesh['genes_0'=4,'genes_1'=4,'genes_2'=2,'genes_3'=2,'cols'=2] {'cols'}, dimensions={0}, use_global_device_ids=true | all-gather | bytes 25200 | tf_op jit(solution)/shard_map/all_gather | solution.py:41
  210.2 0.6 pad_maximum_fusion
  210.8 0.0 copy-done.1
  (21 shorter events, 0.2 us)
Async XLA Ops:
  7.2 6.0 %copy-start = (s32[320,300]{0,1:T(8,128)S(1)}, s32[320,300]{0,1:T(8,128)}, u32[]{:S(2)}) copy-start(s32[320,300]{0,1:T(8,128)} %param.8) | copy-start | bytes 1152004
  7.2 109.3 %all-gather.12.cloned.1.call-start = ((), (), s32[]{:S(2)}) async-start(), calls=%async_computation.3 | async-start | bytes 15974400 | tf_op jit(solution)/shard_map/all_gather | solution.py:114
  35.1 11.2 %all-to-all-start = ((bf16[2,384,320]{1,2,0:T(8,128)(2,1)}), bf16[2,384,320]{1,2,0:T(8,128)(2,1)S(1)}, u32[]{:S(2)}, u32[]{:S(2)}) async-start(bf16[2,384,320]{1,2,0:T(8,128)(2,1)} %broadcast_in_dim.34), calls=%async_computation | async-start | bytes 983040 | tf_op jit(solution)/shard_map/all_to_all | solution.py:21
  116.5 49.9 %copy-start.2 = (f32[320]{0:T(512)S(1)}, f32[320]{0:T(512)}, u32[]{:S(2)}) copy-start(f32[320]{0:T(512)} %param.9) | copy-start | bytes 3844
  161.5 11.2 %all-to-all-start.2 = ((bf16[2,320,300]{1,2,0:T(8,128)(2,1)}), bf16[2,320,300]{1,2,0:T(8,128)(2,1)S(1)}, u32[]{:S(2)}, u32[]{:S(2)}) async-start(bf16[2,320,300]{1,2,0:T(8,128)(2,1)} %copy.25), calls=%async_computation.2 | async-start | bytes 933888 | tf_op jit(solution)/shard_map/all_to_all | solution.py:35
  172.9 37.8 %copy-start.1 = (f32[320,300]{0,1:T(8,128)}, f32[320,300]{0,1:T(8,128)S(1)}, u32[]{:S(2)}) copy-start(f32[320,300]{0,1:T(8,128)S(1)} %get-tuple-element.136) | copy-start | bytes 1152004
Sparse Core Ops, SparseCore 0:
  13.3 103.1 all-gather.11
